TPU v7x, 32 devices: a whole 2x2x4 slice. The times are simulated.
32 devices in a mesh: gx: 4 (over y, x), gy: 8 (over z, core).
Axes of the slice: x: 2, y: 2, z: 4, core: 2. Of those that a mesh axis runs over, the one named last changes fastest.
Arguments:
- traces: bfloat16 [8, 16, 128, 256], P('gx', 'gy'), may hold values from -6 to 6
- aperture: int32 [8, 16, 9], P('gx', 'gy'), may hold values 0 or 1
- geometry: int32 [8, 16, 3, 128], P('gx', 'gy'), may hold values from 0 to 63, as said below
- trace_weight: bfloat16 [8, 16, 128], P('gx', 'gy'), may hold values from 0.0087890625 to 0.03515625
- class_weight: float32 [14], replicated, may hold values from 0.3 to 1.5
- traveltime: int32 [14, 256], replicated, may hold values from 0 to 1114
Outputs:
- image: float32 [64, 64, 256], P('gx', 'gy')
Inputs may be any that keep to these rules, and one draw needn't show every extreme that they name: Row 0 of a trace's geometry is an inline midpoint among the 16 image columns of its block's tile, row 1 a crossline midpoint among its tile's 8 columns, row 2 an offset class below 8.
All inputs are finite; a program needn't handle non-finite values. No bound on the sum of `aperture` on one device may be relied on, other than what follows from the above.
Results may differ from a plain program's by a relative error of at most 0.0029.
Values may be sent and summed in bfloat16 or wider, within the bound.
A program may use at most 64 MiB of HBM per device.

v0:
```python
import jax
import jax.numpy as jnp
from jax import lax
from jax.sharding import PartitionSpec as P

NS = 256
NTIME = 256
PX = 16
PY = 8
DSTEP = 8


def padded(cells, sides, width):
    for axis, dim in sides:
        count = lax.axis_size(axis)
        ends = count - 1
        head = lax.slice_in_dim(cells, 0, width, axis=dim)
        tail = lax.slice_in_dim(cells, cells.shape[dim] - width, cells.shape[dim], axis=dim)
        cells = jnp.concatenate(
            [
                lax.ppermute(tail, axis, [(i, (i + 1) % count) for i in range(ends)]),
                cells,
                lax.ppermute(head, axis, [((i + 1) % count, i) for i in range(ends)]),
            ],
            axis=dim,
        )
    return cells


def migrate(samples_in, live_weights, geometry, tile_x, tile_y, traveltime, class_weight):
    points = jnp.arange(PX * PY, dtype=jnp.int32)
    point_x = tile_x * PX + points // PY
    point_y = tile_y * PY + points % PY
    distance = jnp.abs(point_x[:, None] - geometry[0][None, :]) + jnp.abs(
        point_y[:, None] - geometry[1][None, :]
    )
    classes = geometry[2][None, :] + distance // DSTEP
    sample_ids = jnp.arange(NS, dtype=jnp.int32)[:, None]

    def add_class(level, image):
        scaled = (live_weights * class_weight[level]).astype(jnp.bfloat16)
        amplitude = jnp.where(classes == level, scaled[None, :], jnp.zeros((), jnp.bfloat16))
        stacked = jnp.dot(amplitude, samples_in, preferred_element_type=jnp.float32)
        quarter = traveltime[level]
        first_sample = quarter // 4
        fraction = (quarter % 4).astype(jnp.float32) * 0.25
        interp = jnp.where(
            sample_ids == first_sample[None, :], 1.0 - fraction[None, :], 0.0
        ) + jnp.where(sample_ids == first_sample[None, :] + 1, fraction[None, :], 0.0)
        return image + jnp.dot(
            stacked, interp, precision=lax.Precision.HIGHEST, preferred_element_type=jnp.float32
        )

    return lax.fori_loop(
        0, class_weight.shape[0], add_class, jnp.zeros((PX * PY, NTIME), jnp.float32)
    )


def per_device(traces, aperture, geometry, trace_weight, class_weight, traveltime):
    blocks = traces.shape[0]
    tile_x = lax.axis_index("gx")
    tile_y = lax.axis_index("gy")
    near_traces, near_weight = (
        padded(traces, (("gx", 0), ("gy", 1)), blocks),
        padded(trace_weight, (("gx", 0), ("gy", 1)), blocks),
    )
    near_aperture, near_geometry = (
        padded(aperture, (("gx", 0), ("gy", 1)), blocks),
        padded(geometry, (("gx", 0), ("gy", 1)), blocks),
    )
    offset = jnp.arange(3 * blocks, dtype=jnp.int32) // blocks - 1
    wanted = (1 - offset)[:, None] * 3 + (1 - offset)[None, :]
    choose = (jnp.arange(9, dtype=jnp.int32)[None, None, :] == wanted[:, :, None]).astype(jnp.int32)
    live_block = jnp.sum(near_aperture * choose, axis=2)
    live = jnp.broadcast_to(live_block[:, :, None], near_weight.shape).reshape(-1)
    live_weights = near_weight.reshape(-1).astype(jnp.float32) * live.astype(jnp.float32)
    flat_geometry = jnp.moveaxis(near_geometry, 2, 0).reshape(3, -1)
    image = migrate(
        near_traces.reshape(-1, NS),
        live_weights,
        flat_geometry,
        tile_x,
        tile_y,
        traveltime,
        class_weight,
    )
    return image.reshape(PX, PY, NTIME)


def solution(mesh):
    return jax.shard_map(
        per_device,
        mesh=mesh,
        in_specs=(
            P("gx", "gy", None, None),
            P("gx", "gy", None),
            P("gx", "gy", None, None),
            P("gx", "gy", None),
            P(),
            P(),
        ),
        out_specs=P("gx", "gy", None),
        check_vma=False,
    )
```

profile of v0, /device:TPU:1, one launch (start us, length us, event | category | flops | bytes accessed | tf_op | source)
XLA Modules:
  0.0 140.5 jit_solution(11701377467847930020)
XLA Ops:
  0.0 3.9 %collective-permute-start.8 = (s32[2,2,9]{2,1,0:T(2,128)}, s32[2,2,9]{2,1,0:T(2,128)S(1)}, u32[]{:S(2)}, u32[]{:S(2)}) collective-permute-start(s32[2,2,9]{2,1,0:T(2,128)} %param.9), channel_id=1, source_target_pairs={{0,8},{8,16},{16,24},{1,9},{9,17},{17,25},{2,10},{10,18},{18,26},{... | collective-permute-start | bytes 440 | tf_op jit(solution)/shard_map/ppermute | solution.py:21
  5.2 4.0 %collective-permute-start.4 = (bf16[2,2,128]{2,1,0:T(2,128)(2,1)}, bf16[2,2,128]{2,1,0:T(2,128)(2,1)S(1)}, u32[]{:S(2)}, u32[]{:S(2)}) collective-permute-start(bf16[2,2,128]{2,1,0:T(2,128)(2,1)} %param.11), channel_id=1, source_target_pairs={{0,8},{8,16},{16,24},{1,9},{9,17},{17,25},{2,10},{10,18},{18,26},{... | collective-permute-start | bytes 3080 | tf_op jit(solution)/shard_map/ppermute | solution.py:21
  10.5 4.7 %collective-permute-start = (s32[2,2,3,128]{3,1,2,0:T(2,128)}, s32[2,2,3,128]{3,1,2,0:T(2,128)S(1)}, u32[]{:S(2)}, u32[]{:S(2)}) collective-permute-start(s32[2,2,3,128]{3,1,2,0:T(2,128)} %param.10), channel_id=1, source_target_pairs={{0,8},{8,16},{16,24},{1,9},{9,17},{17,25},{2,10},{10,18},{18,26},{... | collective-permute-start | bytes 18440 | tf_op jit(solution)/shard_map/ppermute | solution.py:21
  16.0 4.9 %collective-permute-start.10 = (s32[6,2,9]{2,1,0:T(2,128)S(1)}, s32[6,2,9]{2,1,0:T(2,128)S(1)}, u32[]{:S(2)}, u32[]{:S(2)}) collective-permute-start(s32[6,2,9]{2,1,0:T(2,128)S(1)} %constant_dynamic-update-slice_fusion.3), channel_id=1, source_target_pairs={{0,1},{1,2},{2,3},{3,4},{4,5},{5,6},{6,7},{8,9},{9,10},{10,11},{11... | collective-permute-start | bytes 1304 | tf_op jit(solution)/shard_map/ppermute | solution.py:21
  25.8 4.5 %collective-permute-start.12 = (bf16[2,2,128,256]{3,2,1,0:T(8,128)(2,1)}, bf16[2,2,128,256]{3,2,1,0:T(8,128)(2,1)S(1)}, u32[]{:S(2)}, u32[]{:S(2)}) collective-permute-start(bf16[2,2,128,256]{3,2,1,0:T(8,128)(2,1)} %param.8), channel_id=1, source_target_pairs={{0,8},{8,16},{16,24},{1,9},{9,17},{17,25},{2,10},{10,18},{18,26},{... | collective-permute-start | bytes 786440 | tf_op jit(solution)/shard_map/ppermute | solution.py:21
  32.7 2.9 %collective-permute-start.6 = (bf16[6,2,128]{2,1,0:T(2,128)(2,1)S(1)}, bf16[6,2,128]{2,1,0:T(2,128)(2,1)S(1)}, u32[]{:S(2)}, u32[]{:S(2)}) collective-permute-start(bf16[6,2,128]{2,1,0:T(2,128)(2,1)S(1)} %constant_dynamic-update-slice_fusion), channel_id=1, source_target_pairs={{0,1},{1,2},{2,3},{3,4},{4,5},{5,6},{6,7},{8,9},{9,10},{10,11},{11... | collective-permute-start | bytes 9224 | tf_op jit(solution)/shard_map/ppermute | solution.py:21
  38.5 3.9 %collective-permute-done.13 = bf16[2,2,128,256]{3,2,1,0:T(8,128)(2,1)S(1)} collective-permute-done((bf16[2,2,128,256]{3,2,1,0:T(8,128)(2,1)}, bf16[2,2,128,256]{3,2,1,0:T(8,128)(2,1)S(1)}, u32[]{:S(2)}, u32[]{:S(2)}) %collective-permute-start.13) | collective-permute-done | bytes 262176 | tf_op jit(solution)/shard_map/ppermute | solution.py:23
  42.4 5.5 %collective-permute-start.14 = (bf16[6,2,128,256]{3,2,1,0:T(8,128)(2,1)S(1)}, bf16[6,2,128,256]{3,2,1,0:T(8,128)(2,1)S(1)}, u32[]{:S(2)}, u32[]{:S(2)}) collective-permute-start(bf16[6,2,128,256]{3,2,1,0:T(8,128)(2,1)S(1)} %constant_dynamic-update-slice_fusion.6), channel_id=1, source_target_pairs={{0,1},{1,2},{2,3},{3,4},{4,5},{5,6},{6,7},{8,9},{9,10},{10,11},{11... | collective-permute-start | bytes 2359304 | tf_op jit(solution)/shard_map/ppermute | solution.py:21
  50.5 3.6 %collective-permute-start.2 = (s32[6,2,3,128]{3,1,2,0:T(2,128)S(1)}, s32[6,2,3,128]{3,1,2,0:T(2,128)S(1)}, u32[]{:S(2)}, u32[]{:S(2)}) collective-permute-start(s32[6,2,3,128]{3,1,2,0:T(2,128)S(1)} %constant_dynamic-update-slice_fusion.9), channel_id=1, source_target_pairs={{0,1},{1,2},{2,3},{3,4},{4,5},{5,6},{6,7},{8,9},{9,10},{10,11},{11... | collective-permute-start | bytes 55304 | tf_op jit(solution)/shard_map/ppermute | solution.py:21
  57.0 4.4 %collective-permute-done.3 = s32[6,2,3,128]{3,1,2,0:T(2,128)S(1)} collective-permute-done((s32[6,2,3,128]{3,1,2,0:T(2,128)S(1)}, s32[6,2,3,128]{3,1,2,0:T(2,128)S(1)}, u32[]{:S(2)}, u32[]{:S(2)}) %collective-permute-start.3) | collective-permute-done | bytes 18464 | tf_op jit(solution)/shard_map/ppermute | solution.py:23
  64.0 75.8 %while.17 = (s32[]{:T(128)}, f32[128,256]{1,0:T(8,128)S(1)}, f32[14]{0:T(128)S(1)}, f32[4608]{0:T(1024)S(1)}, bf16[4608,256]{1,0:T(8,128)(2,1)S(1)}, /*index=5*/...) while((s32[]{:T(128)}, f32[128,256]{1,0:T(8,128)S(1)}, ...), condition=%wide.region_2.3_spmd.clone.clone, body=%wide.region_1.2_spmd.clone.clone.sunk | while | flops 416628480 | bytes 2989219 | solution.py:54
  65.3 2.3 %fusion.60 = f32[128,256]{1,0:T(8,128)S(1)} fusion(bf16[4608,256]{1,0:T(8,128)(2,1)S(1)} %get-tuple-element.416, s32[4608]{0:T(1024)S(1)} %get-tuple-element.420, s32[128]{0:T(128)S(1)} %get-tuple-element.421, s32[4608]{0:T(1024)S(1)} %get-tuple-element.418, s32[128]{0:T(128)S(1)} %get-tuple-element.419, s32[4608]{0:T(1024)S(1)} %get-tuple-element.422, ...), kind=kOutput, calls=%fused_computation.14.clone.1 | convolution fusion | flops 315555840 | bytes 2555908 | tf_op jit(solution)/shard_map/while/body/eval_jaxpr/dot_general | solution.py:43
  70.7 2.3 %fusion.60 = f32[128,256]{1,0:T(8,128)S(1)} fusion(bf16[4608,256]{1,0:T(8,128)(2,1)S(1)} %get-tuple-element.416, s32[4608]{0:T(1024)S(1)} %get-tuple-element.420, s32[128]{0:T(128)S(1)} %get-tuple-element.421, s32[4608]{0:T(1024)S(1)} %get-tuple-element.418, s32[128]{0:T(128)S(1)} %get-tuple-element.419, s32[4608]{0:T(1024)S(1)} %get-tuple-element.422, ...), kind=kOutput, calls=%fused_computation.14.clone.1 | convolution fusion | flops 315555840 | bytes 2555908 | tf_op jit(solution)/shard_map/while/body/eval_jaxpr/dot_general | solution.py:43
  76.1 2.3 %fusion.60 = f32[128,256]{1,0:T(8,128)S(1)} fusion(bf16[4608,256]{1,0:T(8,128)(2,1)S(1)} %get-tuple-element.416, s32[4608]{0:T(1024)S(1)} %get-tuple-element.420, s32[128]{0:T(128)S(1)} %get-tuple-element.421, s32[4608]{0:T(1024)S(1)} %get-tuple-element.418, s32[128]{0:T(128)S(1)} %get-tuple-element.419, s32[4608]{0:T(1024)S(1)} %get-tuple-element.422, ...), kind=kOutput, calls=%fused_computation.14.clone.1 | convolution fusion | flops 315555840 | bytes 2555908 | tf_op jit(solution)/shard_map/while/body/eval_jaxpr/dot_general | solution.py:43
  81.6 2.3 %fusion.60 = f32[128,256]{1,0:T(8,128)S(1)} fusion(bf16[4608,256]{1,0:T(8,128)(2,1)S(1)} %get-tuple-element.416, s32[4608]{0:T(1024)S(1)} %get-tuple-element.420, s32[128]{0:T(128)S(1)} %get-tuple-element.421, s32[4608]{0:T(1024)S(1)} %get-tuple-element.418, s32[128]{0:T(128)S(1)} %get-tuple-element.419, s32[4608]{0:T(1024)S(1)} %get-tuple-element.422, ...), kind=kOutput, calls=%fused_computation.14.clone.1 | convolution fusion | flops 315555840 | bytes 2555908 | tf_op jit(solution)/shard_map/while/body/eval_jaxpr/dot_general | solution.py:43
  87.0 2.3 %fusion.60 = f32[128,256]{1,0:T(8,128)S(1)} fusion(bf16[4608,256]{1,0:T(8,128)(2,1)S(1)} %get-tuple-element.416, s32[4608]{0:T(1024)S(1)} %get-tuple-element.420, s32[128]{0:T(128)S(1)} %get-tuple-element.421, s32[4608]{0:T(1024)S(1)} %get-tuple-element.418, s32[128]{0:T(128)S(1)} %get-tuple-element.419, s32[4608]{0:T(1024)S(1)} %get-tuple-element.422, ...), kind=kOutput, calls=%fused_computation.14.clone.1 | convolution fusion | flops 315555840 | bytes 2555908 | tf_op jit(solution)/shard_map/while/body/eval_jaxpr/dot_general | solution.py:43
  92.4 2.3 %fusion.60 = f32[128,256]{1,0:T(8,128)S(1)} fusion(bf16[4608,256]{1,0:T(8,128)(2,1)S(1)} %get-tuple-element.416, s32[4608]{0:T(1024)S(1)} %get-tuple-element.420, s32[128]{0:T(128)S(1)} %get-tuple-element.421, s32[4608]{0:T(1024)S(1)} %get-tuple-element.418, s32[128]{0:T(128)S(1)} %get-tuple-element.419, s32[4608]{0:T(1024)S(1)} %get-tuple-element.422, ...), kind=kOutput, calls=%fused_computation.14.clone.1 | convolution fusion | flops 315555840 | bytes 2555908 | tf_op jit(solution)/shard_map/while/body/eval_jaxpr/dot_general | solution.py:43
  97.8 2.3 %fusion.60 = f32[128,256]{1,0:T(8,128)S(1)} fusion(bf16[4608,256]{1,0:T(8,128)(2,1)S(1)} %get-tuple-element.416, s32[4608]{0:T(1024)S(1)} %get-tuple-element.420, s32[128]{0:T(128)S(1)} %get-tuple-element.421, s32[4608]{0:T(1024)S(1)} %get-tuple-element.418, s32[128]{0:T(128)S(1)} %get-tuple-element.419, s32[4608]{0:T(1024)S(1)} %get-tuple-element.422, ...), kind=kOutput, calls=%fused_computation.14.clone.1 | convolution fusion | flops 315555840 | bytes 2555908 | tf_op jit(solution)/shard_map/while/body/eval_jaxpr/dot_general | solution.py:43
  103.2 2.3 %fusion.60 = f32[128,256]{1,0:T(8,128)S(1)} fusion(bf16[4608,256]{1,0:T(8,128)(2,1)S(1)} %get-tuple-element.416, s32[4608]{0:T(1024)S(1)} %get-tuple-element.420, s32[128]{0:T(128)S(1)} %get-tuple-element.421, s32[4608]{0:T(1024)S(1)} %get-tuple-element.418, s32[128]{0:T(128)S(1)} %get-tuple-element.419, s32[4608]{0:T(1024)S(1)} %get-tuple-element.422, ...), kind=kOutput, calls=%fused_computation.14.clone.1 | convolution fusion | flops 315555840 | bytes 2555908 | tf_op jit(solution)/shard_map/while/body/eval_jaxpr/dot_general | solution.py:43
  108.6 2.3 %fusion.60 = f32[128,256]{1,0:T(8,128)S(1)} fusion(bf16[4608,256]{1,0:T(8,128)(2,1)S(1)} %get-tuple-element.416, s32[4608]{0:T(1024)S(1)} %get-tuple-element.420, s32[128]{0:T(128)S(1)} %get-tuple-element.421, s32[4608]{0:T(1024)S(1)} %get-tuple-element.418, s32[128]{0:T(128)S(1)} %get-tuple-element.419, s32[4608]{0:T(1024)S(1)} %get-tuple-element.422, ...), kind=kOutput, calls=%fused_computation.14.clone.1 | convolution fusion | flops 315555840 | bytes 2555908 | tf_op jit(solution)/shard_map/while/body/eval_jaxpr/dot_general | solution.py:43
  114.1 2.3 %fusion.60 = f32[128,256]{1,0:T(8,128)S(1)} fusion(bf16[4608,256]{1,0:T(8,128)(2,1)S(1)} %get-tuple-element.416, s32[4608]{0:T(1024)S(1)} %get-tuple-element.420, s32[128]{0:T(128)S(1)} %get-tuple-element.421, s32[4608]{0:T(1024)S(1)} %get-tuple-element.418, s32[128]{0:T(128)S(1)} %get-tuple-element.419, s32[4608]{0:T(1024)S(1)} %get-tuple-element.422, ...), kind=kOutput, calls=%fused_computation.14.clone.1 | convolution fusion | flops 315555840 | bytes 2555908 | tf_op jit(solution)/shard_map/while/body/eval_jaxpr/dot_general | solution.py:43
  119.5 2.3 %fusion.60 = f32[128,256]{1,0:T(8,128)S(1)} fusion(bf16[4608,256]{1,0:T(8,128)(2,1)S(1)} %get-tuple-element.416, s32[4608]{0:T(1024)S(1)} %get-tuple-element.420, s32[128]{0:T(128)S(1)} %get-tuple-element.421, s32[4608]{0:T(1024)S(1)} %get-tuple-element.418, s32[128]{0:T(128)S(1)} %get-tuple-element.419, s32[4608]{0:T(1024)S(1)} %get-tuple-element.422, ...), kind=kOutput, calls=%fused_computation.14.clone.1 | convolution fusion | flops 315555840 | bytes 2555908 | tf_op jit(solution)/shard_map/while/body/eval_jaxpr/dot_general | solution.py:43
  124.9 2.3 %fusion.60 = f32[128,256]{1,0:T(8,128)S(1)} fusion(bf16[4608,256]{1,0:T(8,128)(2,1)S(1)} %get-tuple-element.416, s32[4608]{0:T(1024)S(1)} %get-tuple-element.420, s32[128]{0:T(128)S(1)} %get-tuple-element.421, s32[4608]{0:T(1024)S(1)} %get-tuple-element.418, s32[128]{0:T(128)S(1)} %get-tuple-element.419, s32[4608]{0:T(1024)S(1)} %get-tuple-element.422, ...), kind=kOutput, calls=%fused_computation.14.clone.1 | convolution fusion | flops 315555840 | bytes 2555908 | tf_op jit(solution)/shard_map/while/body/eval_jaxpr/dot_general | solution.py:43
  135.7 2.3 %fusion.60 = f32[128,256]{1,0:T(8,128)S(1)} fusion(bf16[4608,256]{1,0:T(8,128)(2,1)S(1)} %get-tuple-element.416, s32[4608]{0:T(1024)S(1)} %get-tuple-element.420, s32[128]{0:T(128)S(1)} %get-tuple-element.421, s32[4608]{0:T(1024)S(1)} %get-tuple-element.418, s32[128]{0:T(128)S(1)} %get-tuple-element.419, s32[4608]{0:T(1024)S(1)} %get-tuple-element.422, ...), kind=kOutput, calls=%fused_computation.14.clone.1 | convolution fusion | flops 315555840 | bytes 2555908 | tf_op jit(solution)/shard_map/while/body/eval_jaxpr/dot_general | solution.py:43
  (125 shorter events, 67.4 us)
Async XLA Ops:
  0.0 15.3 %collective-permute-start.8 = (s32[2,2,9]{2,1,0:T(2,128)}, s32[2,2,9]{2,1,0:T(2,128)S(1)}, u32[]{:S(2)}, u32[]{:S(2)}) collective-permute-start(s32[2,2,9]{2,1,0:T(2,128)} %param.9), channel_id=1, source_target_pairs={{0,8},{8,16},{16,24},{1,9},{9,17},{17,25},{2,10},{10,18},{18,26},{... | collective-permute-start | bytes 440 | tf_op jit(solution)/shard_map/ppermute | solution.py:21
  3.9 12.0 %collective-permute-start.9 = (s32[2,2,9]{2,1,0:T(2,128)}, s32[2,2,9]{2,1,0:T(2,128)S(1)}, u32[]{:S(2)}, u32[]{:S(2)}) collective-permute-start(s32[2,2,9]{2,1,0:T(2,128)} %param.9), channel_id=1, source_target_pairs={{8,0},{16,8},{24,16},{9,1},{17,9},{25,17},{10,2},{18,10},{26,18},{... | collective-permute-start | bytes 440 | tf_op jit(solution)/shard_map/ppermute | solution.py:23
  5.2 25.4 %collective-permute-start.4 = (bf16[2,2,128]{2,1,0:T(2,128)(2,1)}, bf16[2,2,128]{2,1,0:T(2,128)(2,1)S(1)}, u32[]{:S(2)}, u32[]{:S(2)}) collective-permute-start(bf16[2,2,128]{2,1,0:T(2,128)(2,1)} %param.11), channel_id=1, source_target_pairs={{0,8},{8,16},{16,24},{1,9},{9,17},{17,25},{2,10},{10,18},{18,26},{... | collective-permute-start | bytes 3080 | tf_op jit(solution)/shard_map/ppermute | solution.py:21
  9.2 23.4 %collective-permute-start.5 = (bf16[2,2,128]{2,1,0:T(2,128)(2,1)}, bf16[2,2,128]{2,1,0:T(2,128)(2,1)S(1)}, u32[]{:S(2)}, u32[]{:S(2)}) collective-permute-start(bf16[2,2,128]{2,1,0:T(2,128)(2,1)} %param.11), channel_id=1, source_target_pairs={{8,0},{16,8},{24,16},{9,1},{17,9},{25,17},{10,2},{18,10},{26,18},{... | collective-permute-start | bytes 3080 | tf_op jit(solution)/shard_map/ppermute | solution.py:23
  10.5 25.0 %collective-permute-start = (s32[2,2,3,128]{3,1,2,0:T(2,128)}, s32[2,2,3,128]{3,1,2,0:T(2,128)S(1)}, u32[]{:S(2)}, u32[]{:S(2)}) collective-permute-start(s32[2,2,3,128]{3,1,2,0:T(2,128)} %param.10), channel_id=1, source_target_pairs={{0,8},{8,16},{16,24},{1,9},{9,17},{17,25},{2,10},{10,18},{18,26},{... | collective-permute-start | bytes 18440 | tf_op jit(solution)/shard_map/ppermute | solution.py:21
  16.0 6.8 %collective-permute-start.10 = (s32[6,2,9]{2,1,0:T(2,128)S(1)}, s32[6,2,9]{2,1,0:T(2,128)S(1)}, u32[]{:S(2)}, u32[]{:S(2)}) collective-permute-start(s32[6,2,9]{2,1,0:T(2,128)S(1)} %constant_dynamic-update-slice_fusion.3), channel_id=1, source_target_pairs={{0,1},{1,2},{2,3},{3,4},{4,5},{5,6},{6,7},{8,9},{9,10},{10,11},{11... | collective-permute-start | bytes 1304 | tf_op jit(solution)/shard_map/ppermute | solution.py:21
  20.9 4.9 %collective-permute-start.11 = (s32[6,2,9]{2,1,0:T(2,128)S(1)}, s32[6,2,9]{2,1,0:T(2,128)S(1)}, u32[]{:S(2)}, u32[]{:S(2)}) collective-permute-start(s32[6,2,9]{2,1,0:T(2,128)S(1)} %constant_dynamic-update-slice_fusion.3), channel_id=1, source_target_pairs={{1,0},{2,1},{3,2},{4,3},{5,4},{6,5},{7,6},{9,8},{10,9},{11,10},{12... | collective-permute-start | bytes 1304 | tf_op jit(solution)/shard_map/ppermute | solution.py:23
  22.8 27.7 %collective-permute-start.1 = (s32[2,2,3,128]{3,1,2,0:T(2,128)}, s32[2,2,3,128]{3,1,2,0:T(2,128)S(1)}, u32[]{:S(2)}, u32[]{:S(2)}) collective-permute-start(s32[2,2,3,128]{3,1,2,0:T(2,128)} %param.10), channel_id=1, source_target_pairs={{8,0},{16,8},{24,16},{9,1},{17,9},{25,17},{10,2},{18,10},{26,18},{... | collective-permute-start | bytes 18440 | tf_op jit(solution)/shard_map/ppermute | solution.py:23
  25.8 11.7 %collective-permute-start.12 = (bf16[2,2,128,256]{3,2,1,0:T(8,128)(2,1)}, bf16[2,2,128,256]{3,2,1,0:T(8,128)(2,1)S(1)}, u32[]{:S(2)}, u32[]{:S(2)}) collective-permute-start(bf16[2,2,128,256]{3,2,1,0:T(8,128)(2,1)} %param.8), channel_id=1, source_target_pairs={{0,8},{8,16},{16,24},{1,9},{9,17},{17,25},{2,10},{10,18},{18,26},{... | collective-permute-start | bytes 786440 | tf_op jit(solution)/shard_map/ppermute | solution.py:21
  30.6 11.7 %collective-permute-start.13 = (bf16[2,2,128,256]{3,2,1,0:T(8,128)(2,1)}, bf16[2,2,128,256]{3,2,1,0:T(8,128)(2,1)S(1)}, u32[]{:S(2)}, u32[]{:S(2)}) collective-permute-start(bf16[2,2,128,256]{3,2,1,0:T(8,128)(2,1)} %param.8), channel_id=1, source_target_pairs={{8,0},{16,8},{24,16},{9,1},{17,9},{25,17},{10,2},{18,10},{26,18},{... | collective-permute-start | bytes 786440 | tf_op jit(solution)/shard_map/ppermute | solution.py:23
  32.7 21.5 %collective-permute-start.6 = (bf16[6,2,128]{2,1,0:T(2,128)(2,1)S(1)}, bf16[6,2,128]{2,1,0:T(2,128)(2,1)S(1)}, u32[]{:S(2)}, u32[]{:S(2)}) collective-permute-start(bf16[6,2,128]{2,1,0:T(2,128)(2,1)S(1)} %constant_dynamic-update-slice_fusion), channel_id=1, source_target_pairs={{0,1},{1,2},{2,3},{3,4},{4,5},{5,6},{6,7},{8,9},{9,10},{10,11},{11... | collective-permute-start | bytes 9224 | tf_op jit(solution)/shard_map/ppermute | solution.py:21
  35.6 20.5 %collective-permute-start.7 = (bf16[6,2,128]{2,1,0:T(2,128)(2,1)S(1)}, bf16[6,2,128]{2,1,0:T(2,128)(2,1)S(1)}, u32[]{:S(2)}, u32[]{:S(2)}) collective-permute-start(bf16[6,2,128]{2,1,0:T(2,128)(2,1)S(1)} %constant_dynamic-update-slice_fusion), channel_id=1, source_target_pairs={{1,0},{2,1},{3,2},{4,3},{5,4},{6,5},{7,6},{9,8},{10,9},{11,10},{12... | collective-permute-start | bytes 9224 | tf_op jit(solution)/shard_map/ppermute | solution.py:23
  42.4 19.1 %collective-permute-start.14 = (bf16[6,2,128,256]{3,2,1,0:T(8,128)(2,1)S(1)}, bf16[6,2,128,256]{3,2,1,0:T(8,128)(2,1)S(1)}, u32[]{:S(2)}, u32[]{:S(2)}) collective-permute-start(bf16[6,2,128,256]{3,2,1,0:T(8,128)(2,1)S(1)} %constant_dynamic-update-slice_fusion.6), channel_id=1, source_target_pairs={{0,1},{1,2},{2,3},{3,4},{4,5},{5,6},{6,7},{8,9},{9,10},{10,11},{11... | collective-permute-start | bytes 2359304 | tf_op jit(solution)/shard_map/ppermute | solution.py:21
  47.9 14.5 %collective-permute-start.15 = (bf16[6,2,128,256]{3,2,1,0:T(8,128)(2,1)S(1)}, bf16[6,2,128,256]{3,2,1,0:T(8,128)(2,1)}, u32[]{:S(2)}, u32[]{:S(2)}) collective-permute-start(bf16[6,2,128,256]{3,2,1,0:T(8,128)(2,1)S(1)} %constant_dynamic-update-slice_fusion.6), channel_id=1, source_target_pairs={{1,0},{2,1},{3,2},{4,3},{5,4},{6,5},{7,6},{9,8},{10,9},{11,10},{12... | collective-permute-start | bytes 2359304 | tf_op jit(solution)/shard_map/ppermute | solution.py:23
  50.5 6.5 %collective-permute-start.2 = (s32[6,2,3,128]{3,1,2,0:T(2,128)S(1)}, s32[6,2,3,128]{3,1,2,0:T(2,128)S(1)}, u32[]{:S(2)}, u32[]{:S(2)}) collective-permute-start(s32[6,2,3,128]{3,1,2,0:T(2,128)S(1)} %constant_dynamic-update-slice_fusion.9), channel_id=1, source_target_pairs={{0,1},{1,2},{2,3},{3,4},{4,5},{5,6},{6,7},{8,9},{9,10},{10,11},{11... | collective-permute-start | bytes 55304 | tf_op jit(solution)/shard_map/ppermute | solution.py:21
  54.2 7.2 %collective-permute-start.3 = (s32[6,2,3,128]{3,1,2,0:T(2,128)S(1)}, s32[6,2,3,128]{3,1,2,0:T(2,128)S(1)}, u32[]{:S(2)}, u32[]{:S(2)}) collective-permute-start(s32[6,2,3,128]{3,1,2,0:T(2,128)S(1)} %constant_dynamic-update-slice_fusion.9), channel_id=1, source_target_pairs={{1,0},{2,1},{3,2},{4,3},{5,4},{6,5},{7,6},{9,8},{10,9},{11,10},{12... | collective-permute-start | bytes 55304 | tf_op jit(solution)/shard_map/ppermute | solution.py:23
  61.5 2.6 %copy-start.1 = (f32[14]{0:T(128)S(1)}, f32[14]{0:T(128)}, u32[]{:S(2)}) copy-start(f32[14]{0:T(128)} %param.12) | copy-start | bytes 172
  61.5 0.9 copy-start
  139.9 0.7 copy-start.2
where the time goes:
time: 143 us; the launch traced here: 141 us
  starting transfers between devices  46.8 us (33%)
  matrix products  37.4 us (26%)
  other arithmetic  31.2 us (22%)
  local copies, waits for them, and re-layouts  13.4 us (9%)
  waiting for transfers between devices  10.8 us (8%)
    ppermute x8, starting transfers between devices, padded(): lax.ppermute(tail, axis, [(i, (i + 1) % count) for i in range(ends)])  34 us
    dot_general x14, matrix products, add_class(): stacked = jnp.dot(amplitude, samples_in, preferred_element_type=jnp.float32)  32.2 us
    ppermute x8, starting transfers between devices, padded(): lax.ppermute(head, axis, [((i + 1) % count, i) for i in range(ends)])  12.9 us
    sub x14, other arithmetic, add_class(): 1.0 - fraction[None, :]  10.3 us
    add x14, other arithmetic, add_class(): first_sample[None, :] + 1  10 us
    ppermute x8, waiting for transfers between devices, padded(): lax.ppermute(head, axis, [((i + 1) % count, i) for i in range(ends)])  9.95 us
    convert_element_type x14, other arithmetic, add_class(): scaled = (live_weights * class_weight[level]).astype(jnp.bfloat16)  8.83 us
    dynamic_slice x14, local copies, waits for them, and re-layouts, add_class(): scaled = (live_weights * class_weight[level]).astype(jnp.bfloat16)  8.68 us
  transfers between devices with their start and end apart: 16, of which 4 were waited for; matrix products, arithmetic and copies ran while one was open for 3% of the time, Pallas kernels for 0%

commit v1 on v0

v1 whole, which is shorter than its diff:
```python
import functools

import jax
import jax.numpy as jnp
from jax import lax
from jax.experimental import pallas as pl
from jax.experimental.pallas import tpu as pltpu
from jax.sharding import PartitionSpec as P

PX = 16
PY = 8
DSTEP = 8
MESH = pl.DeviceIdType.MESH
BF = jnp.bfloat16
F32 = jnp.float32

ND = (2 * PX - 1 + 2 * PY - 1) // DSTEP + 1


def classes_at(dx, dy):
    far_x = 2 * PX - 1 if dx else PX - 1
    far_y = 2 * PY - 1 if dy else PY - 1
    return (far_x + far_y) // DSTEP + 1


def kernel(
    n_x, n_y, traces, geometry, weight, traveltime, aperture, class_weight, image,
    taps, values, amplitude, diag_out, side_out, x_out, diag_in, side_in, x_in,
    send_sem, recv_sem,
):
    bx, by, tr, ns = traces.shape
    nc, nt = traveltime.shape
    nj = bx * by * tr
    cols = PX * PY
    nh = nc - ND + 1
    me_x = lax.axis_index("gx")
    me_y = lax.axis_index("gy")
    has = {
        ("gx", -1): me_x > 0,
        ("gx", 1): me_x < n_x - 1,
        ("gy", -1): me_y > 0,
        ("gy", 1): me_y < n_y - 1,
    }
    at = {"gx": me_x, "gy": me_y}
    sides = ((0, -1), (1, 1))

    barrier = pltpu.get_barrier_semaphore()
    for (axis, step), there in has.items():
        @pl.when(there)
        def _(axis=axis, step=step):
            pl.semaphore_signal(
                barrier, inc=1, device_id={axis: at[axis] + step}, device_id_type=MESH
            )

    def copy(src, dst, number, axis, step):
        return pltpu.make_async_remote_copy(
            src_ref=src, dst_ref=dst,
            send_sem=send_sem.at[number], recv_sem=recv_sem.at[number],
            device_id={axis: at[axis] + step}, device_id_type=MESH,
        )

    diag = [copy(diag_out.at[k], diag_in.at[k], k, "gy", s) for k, s in sides]
    side = [copy(side_out.at[k], side_in.at[k], 2 + k, "gy", s) for k, s in sides]
    across = [copy(x_out.at[k], x_in.at[k], 4 + k, "gx", s) for k, s in sides]

    def start(copies, axis):
        for k, s in sides:
            @pl.when(has[axis, s])
            def _(k=k):
                copies[k].start()

    def arrive(copies, axis, landed):
        for k, s in sides:
            @pl.when(has[axis, -s])
            def _(k=k):
                copies[k].wait_recv()

            @pl.when(jnp.logical_not(has[axis, -s]))
            def _(k=k):
                landed[k] = jnp.zeros(landed.shape[1:], landed.dtype)

    def sent(copies, axis):
        for k, s in sides:
            @pl.when(has[axis, s])
            def _(k=k):
                copies[k].wait_send()

    blocks = [(i, k) for i in range(bx) for k in range(by)]

    def row(ref, r):
        return jnp.concatenate([ref[i, k, r : r + 1, :] for i, k in blocks], axis=1)

    samples = traces[...].reshape(nj, ns)
    sample_ids = lax.broadcasted_iota(jnp.int32, (ns, nt), 0).astype(F32).astype(BF)
    quarter = traveltime[...]
    first = (quarter >> 2).astype(F32)
    fraction = (quarter & 3).astype(F32) * 0.25
    first_b, next_b = first.astype(BF), (first + 1.0).astype(BF)
    frac_b, rest_b = fraction.astype(BF), (1.0 - fraction).astype(BF)
    zero = jnp.zeros((), BF)
    for c in range(nc):
        interp = jnp.where(
            sample_ids == first_b[c : c + 1, :],
            rest_b[c : c + 1, :],
            jnp.where(sample_ids == next_b[c : c + 1, :], frac_b[c : c + 1, :], zero),
        )
        taps[c] = jnp.dot(samples, interp, preferred_element_type=F32).astype(BF)

    for b, (i, k) in enumerate(blocks):
        offset_row = geometry[i, k, 2:3, :].astype(F32)
        offset_col = jnp.broadcast_to(offset_row, (tr, tr)).T.astype(BF)
        for r in range(0, tr, 16):
            rows = pl.ds(b * tr + r, 16)
            o = offset_col[r : r + 16, :]
            o = jnp.concatenate([o] * (nt // tr), axis=1)
            at_class = [taps[c, rows, :] for c in range(nc)]
            is_offset = [o == BF(h) for h in range(nh)]
            for d in range(ND):
                value = at_class[d]
                for h in range(1, nh):
                    value = jnp.where(is_offset[h], at_class[d + h], value)
                values[pl.ds(d * nj + b * tr + r, 16), :] = value

    offset = row(geometry, 2)
    trace_weight = jnp.concatenate([weight[i, k : k + 1, :] for i, k in blocks], axis=1).astype(F32)
    scaled = []
    for d in range(ND):
        factor = jnp.zeros((1, nj), F32)
        for h in range(nh):
            factor = jnp.where(offset == h, class_weight[h + d], factor)
        scaled.append((trace_weight * factor).astype(BF).astype(F32))

    point = lax.broadcasted_iota(jnp.int32, (cols, nj), 0)
    point_x = (point // PY).astype(F32).astype(BF)
    point_y = (point % PY).astype(F32).astype(BF)
    mid_x = (row(geometry, 0) - me_x * PX).astype(F32)
    mid_y = (row(geometry, 1) - me_y * PY).astype(F32)
    grid = 136.0
    shift = (DSTEP - 1) / (2 * DSTEP)
    away_x = {
        dx: jnp.abs(point_x - (mid_x - dx * PX).astype(BF)) * BF(1 / DSTEP) for dx in (-1, 0, 1)
    }
    away_y = {
        dy: jnp.abs(point_y - (mid_y - dy * PY).astype(BF)) * BF(1 / DSTEP) - BF(shift)
        for dy in (-1, 0, 1)
    }

    def migrate(tiles):
        depth = classes_at(*tiles[0]) * nj
        for n, (dx, dy) in enumerate(tiles):
            level = (away_x[dx] + away_y[dy]) + BF(grid)
            entry = (dx + 1) * 3 + (dy + 1)
            live = jnp.concatenate(
                [jnp.full((1, tr), aperture[i, k, entry], jnp.int32) for i, k in blocks], axis=1
            ).astype(F32)
            for d in range(classes_at(dx, dy)):
                amplitude[pl.ds(n * cols, cols), pl.ds(d * nj, nj)] = jnp.where(
                    level == BF(grid + d), (scaled[d] * live).astype(BF), zero
                )
        part = jnp.dot(
            amplitude[pl.ds(0, len(tiles) * cols), pl.ds(0, depth)],
            values[pl.ds(0, depth), :],
            preferred_element_type=F32,
        )
        return [part[n * cols : (n + 1) * cols] for n in range(len(tiles))]

    parts = migrate([(-1, -1), (1, -1), (-1, 1), (1, 1)])
    for n in range(4):
        diag_out[n // 2, n % 2] = parts[n].astype(BF)
    pl.semaphore_wait(barrier, sum(there.astype(jnp.int32) for there in has.values()))
    start(diag, "gy")
    parts = migrate([(0, -1), (0, 1)])
    for n in range(2):
        side_out[n] = parts[n].astype(BF)
    start(side, "gy")
    parts = migrate([(-1, 0), (1, 0)])
    arrive(diag, "gy", diag_in)
    for n in range(2):
        x_out[n] = (parts[n] + diag_in[0, n].astype(F32) + diag_in[1, n].astype(F32)).astype(BF)
    start(across, "gx")
    parts = migrate([(0, 0)])
    arrive(side, "gy", side_in)
    total = parts[0] + side_in[0].astype(F32) + side_in[1].astype(F32)
    arrive(across, "gx", x_in)
    image[...] = total + x_in[0].astype(F32) + x_in[1].astype(F32)
    sent(diag, "gy")
    sent(side, "gy")
    sent(across, "gx")


def per_device(n_x, n_y, traces, aperture, geometry, trace_weight, class_weight, traveltime):
    bx, by, tr, ns = traces.shape
    nc, nt = traveltime.shape
    nj = bx * by * tr
    cols = PX * PY
    vmem = pl.BlockSpec(memory_space=pltpu.VMEM)
    smem = pl.BlockSpec(memory_space=pltpu.SMEM)
    image = pl.pallas_call(
        functools.partial(kernel, n_x, n_y),
        out_shape=jax.ShapeDtypeStruct((cols, nt), F32),
        in_specs=[vmem] * 4 + [smem] * 2,
        out_specs=vmem,
        scratch_shapes=[
            pltpu.VMEM((nc, nj, nt), BF),
            pltpu.VMEM((ND * nj, nt), BF),
            pltpu.VMEM((4 * cols, ND * nj), BF),
            pltpu.VMEM((2, 2, cols, nt), BF),
            pltpu.VMEM((2, cols, nt), BF),
            pltpu.VMEM((2, cols, nt), BF),
            pltpu.VMEM((2, 2, cols, nt), BF),
            pltpu.VMEM((2, cols, nt), BF),
            pltpu.VMEM((2, cols, nt), BF),
            pltpu.SemaphoreType.DMA((6,)),
            pltpu.SemaphoreType.DMA((6,)),
        ],
        compiler_params=pltpu.CompilerParams(collective_id=0, has_side_effects=True),
    )(traces, geometry, trace_weight, traveltime, aperture, class_weight)
    return image.reshape(PX, PY, nt)


def solution(mesh):
    return jax.shard_map(
        functools.partial(per_device, mesh.shape["gx"], mesh.shape["gy"]),
        mesh=mesh,
        in_specs=(
            P("gx", "gy", None, None),
            P("gx", "gy", None),
            P("gx", "gy", None, None),
            P("gx", "gy", None),
            P(),
            P(),
        ),
        out_specs=P("gx", "gy", None),
        check_vma=False,
    )
```

time: 143 us -> 16.4 us (0.11); the launches traced: 141 us -> 16.1 us
  starting transfers between devices: 46.8 us -> 0 us
  matrix products: 37.4 us -> 0 us
  other arithmetic: 31.2 us -> 0 us
  Pallas kernels: 0 us -> 13.2 us
  waiting for transfers between devices: 10.8 us -> 0 us
  local copies, waits for them, and re-layouts: 13.4 us -> 2.86 us
    ppermute x16 -> x0, starting transfers between devices: 46.8 us -> none  [the longest x8 34 us: padded(): lax.ppermute(tail, axis, [(i, (i + 1) % count) for i in range(ends)])]
    dot_general x28 -> x0, matrix products: 37.4 us -> none  [the longest x14 32.2 us: add_class(): stacked = jnp.dot(amplitude, samples_in, preferred_element_type=jnp.float32)]
    pallas_call x0 -> x1, Pallas kernels: none -> 13.2 us  [per_device(): pl.pallas_call(functools.partial(kernel, n_x, n_y), out_shape=jax.ShapeDt...]
    ppermute x16 -> x0, waiting for transfers between devices: 10.8 us -> none  [the longest x8 9.95 us: padded(): lax.ppermute(head, axis, [((i + 1) % count, i) for i in range(ends)])]
    sub x15 -> x0, other arithmetic: 10.3 us -> none  [the longest x14 10.3 us: add_class(): 1.0 - fraction[None, :]]
    add x16 -> x0, other arithmetic: 10.1 us -> none  [the longest x14 10 us: add_class(): first_sample[None, :] + 1]
    convert_element_type x15 -> x0, other arithmetic: 8.84 us -> none  [the longest x14 8.83 us: add_class(): scaled = (live_weights * class_weight[level]).astype(jnp.bfloat16)]
    dynamic_slice x14 -> x0, local copies, waits for them, and re-layouts: 8.68 us -> none  [add_class(): scaled = (live_weights * class_weight[level]).astype(jnp.bfloat16)]
  transfers between devices with their start and end apart: 16 -> 0, of which waited for: 4 -> 0; matrix products, arithmetic and copies ran while one was open for 3% -> 0% of each run, Pallas kernels for 0% -> 0%
where the time goes in v1:
time: 16.4 us; the launch traced here: 16.1 us
  Pallas kernels  13.2 us (80%)
  local copies, waits for them, and re-layouts  2.86 us (17%)
    pallas_call x1, Pallas kernels, per_device(): pl.pallas_call(functools.partial(kernel, n_x, n_y), out_shape=jax.ShapeDt...  13.2 us
    unnamed x2, local copies, waits for them, and re-layouts  2.86 us

profile of v1, /device:TPU:1, one launch (start us, length us, event | category | flops | bytes accessed | tf_op | source)
XLA Modules:
  0.0 16.1 jit_solution(10994414303390634823)
XLA Ops:
  0.0 1.3 %copy.7.geometry = s32[2,2,3,128]{3,2,1,0:T(4,128)} copy(s32[2,2,3,128]{3,1,2,0:T(2,128)} %param.8) | data formatting | bytes 12288 | tf_op args[2]
  1.3 13.2 %shard_map.64 = f32[128,256]{1,0:T(8,128)} custom-call(bf16[2,2,128,256]{3,2,1,0:T(8,128)(2,1)} %traces.1, s32[2,2,3,128]{3,2,1,0:T(4,128)} %copy.7.geometry, bf16[2,2,128]{2,1,0:T(2,128)(2,1)} %weight.1, s32[14,256]{1,0:T(8,128)} %traveltime.1, s32[2,2,9]{2,1,0:T(2,128)} %aperture.1, f32[14]{0:T(128)} %class_weight.1), custom_call_target="tpu_custom_call" | custom-call | tf_op jit(solution)/shard_map/pallas_call | solution.py:198
  14.5 1.6 %copy.9 = f32[16,8,256]{2,1,0:T(8,128)} copy(f32[16,8,256]{2,1,0:T(8,128)} %bitcast.1) | data formatting | bytes 262144

commit v2 on v1

v2 whole, which is shorter than its diff:
```python
import functools

import jax
import jax.numpy as jnp
from jax import lax
from jax.experimental import pallas as pl
from jax.experimental.pallas import tpu as pltpu
from jax.sharding import PartitionSpec as P

PX = 16
PY = 8
DSTEP = 8
MESH = pl.DeviceIdType.MESH
BF = jnp.bfloat16
F32 = jnp.float32

ND = (2 * PX - 1 + 2 * PY - 1) // DSTEP + 1


def classes_at(dx, dy):
    far_x = 2 * PX - 1 if dx else PX - 1
    far_y = 2 * PY - 1 if dy else PY - 1
    return (far_x + far_y) // DSTEP + 1


def kernel(
    n_x, n_y, traces_at, geometry_at, weight_at, traveltime_at, aperture_at, class_weight_at,
    total, from_x, traces, geometry, weight, traveltime, aperture, class_weight,
    interp, taps, values, amplitude, own, y_out, y_in, x_out, x_in,
    load_sem, send_sem, recv_sem,
):
    loads = [
        pltpu.make_async_copy(src, dst, load_sem.at[n])
        for n, (src, dst) in enumerate(
            (
                (traveltime_at, traveltime), (traces_at, traces), (geometry_at, geometry),
                (weight_at, weight), (aperture_at, aperture), (class_weight_at, class_weight),
            )
        )
    ]
    for load in loads:
        load.start()
    bx, by, tr, ns = traces.shape
    nc, nt = traveltime.shape
    nj = bx * by * tr
    cols = PX * PY
    nh = nc - ND + 1
    me_x = lax.axis_index("gx")
    me_y = lax.axis_index("gy")
    turn = 2 * lax.rem(me_x, 2) - 1
    step_x = (turn, -turn)
    step_y = (-1, 1)
    has_x = [jnp.logical_and(me_x + s >= 0, me_x + s < n_x) for s in step_x]
    has_y = [me_y > 0, me_y < n_y - 1]
    barrier = pltpu.get_barrier_semaphore()
    for k in range(2):
        @pl.when(has_x[k])
        def _(k=k):
            pl.semaphore_signal(
                barrier, inc=1, device_id={"gx": me_x + step_x[k]}, device_id_type=MESH
            )

        @pl.when(has_y[k])
        def _(k=k):
            pl.semaphore_signal(
                barrier, inc=1, device_id={"gy": me_y + step_y[k]}, device_id_type=MESH
            )

    def copy(src, dst, number, device):
        return pltpu.make_async_remote_copy(
            src_ref=src, dst_ref=dst,
            send_sem=send_sem.at[number], recv_sem=recv_sem.at[number],
            device_id=device, device_id_type=MESH,
        )

    along_y = [
        [copy(y_out.at[n, k], y_in.at[n, k], 2 * n + k, {"gy": me_y + step_y[k]}) for k in range(2)]
        for n in range(3)
    ]
    along_x = [
        copy(x_out.at[k], x_in.at[k], 6 + k, {"gx": me_x + step_x[k]}) for k in range(2)
    ]

    def when(there, act):
        pl.when(there)(act)

    def send_y(n):
        for k in range(2):
            when(has_y[k], along_y[n][k].start)

    def arrive_y(n):
        for k in range(2):
            when(has_y[1 - k], along_y[n][k].wait_recv)

    for k in range(2):
        @pl.when(jnp.logical_not(has_y[1 - k]))
        def _(k=k):
            for n in range(3):
                y_in[n, k] = jnp.zeros(y_in.shape[2:], BF)

        @pl.when(jnp.logical_not(has_x[k]))
        def _(k=k):
            x_in[k] = jnp.zeros(x_in.shape[1:], BF)

    blocks = [(i, k) for i in range(bx) for k in range(by)]

    def row(ref, r):
        return jnp.concatenate([ref[i, r, k : k + 1, :] for i, k in blocks], axis=1)

    sample_ids = lax.broadcasted_iota(jnp.int32, (ns, nt), 0).astype(F32).astype(BF)
    zero = jnp.zeros((), BF)
    loads[0].wait()
    quarter = traveltime[...]
    first = (quarter >> 2).astype(F32)
    fraction = (quarter & 3).astype(F32) * 0.25
    first_b, next_b = first.astype(BF), (first + 1.0).astype(BF)
    frac_b, rest_b = fraction.astype(BF), (1.0 - fraction).astype(BF)
    for c in range(nc):
        interp[c] = jnp.where(
            sample_ids == first_b[c : c + 1, :],
            rest_b[c : c + 1, :],
            jnp.where(sample_ids == next_b[c : c + 1, :], frac_b[c : c + 1, :], zero),
        )

    for load in loads[1:]:
        load.wait()
    samples = traces[...].reshape(nj, ns)
    for c in range(nc):
        taps[c] = jnp.dot(samples, interp[c], preferred_element_type=F32).astype(BF)

    for b, (i, k) in enumerate(blocks):
        offset_row = geometry[i, 2, k : k + 1, :].astype(F32)
        offset_col = jnp.broadcast_to(offset_row, (tr, tr)).T.astype(BF)
        for r in range(0, tr, 16):
            rows = pl.ds(b * tr + r, 16)
            o = offset_col[r : r + 16, :]
            value = at_class = [
                [taps[c, rows, pl.ds(t, tr)] for t in range(0, nt, tr)] for c in range(nc)
            ]
            is_last = o == BF(nh - 1)
            bit = 1
            while 2 * bit < nh - 1:
                bit *= 2
            while bit:
                digit = o >= BF(bit)
                o = jnp.where(digit, o - BF(bit), o)
                value = [
                    [jnp.where(digit, high, low) for high, low in zip(value[c + bit], value[c])]
                    for c in range(ND + bit - 1)
                ]
                bit //= 2
            value[ND - 1] = [
                jnp.where(is_last, last, v) for last, v in zip(at_class[nc - 1], value[ND - 1])
            ]
            for d in range(ND):
                for n, v in enumerate(value[d]):
                    values[pl.ds(d * nj + b * tr + r, 16), pl.ds(n * tr, tr)] = v

    offset = row(geometry, 2)
    trace_weight = jnp.concatenate([weight[i, k : k + 1, :] for i, k in blocks], axis=1).astype(F32)
    scaled = []
    for d in range(ND):
        factor = jnp.zeros((1, nj), F32)
        for h in range(nh):
            factor = jnp.where(offset == h, class_weight[h + d], factor)
        scaled.append((trace_weight * factor).astype(BF).astype(F32))

    point = lax.broadcasted_iota(jnp.int32, (cols, nj), 0)
    point_x = (point // PY).astype(F32).astype(BF)
    point_y = (point % PY).astype(F32).astype(BF)
    mid_x = row(geometry, 0) - me_x * PX
    mid_y = row(geometry, 1) - me_y * PY
    grid = 136.0
    shift = (DSTEP - 1) / (2 * DSTEP)
    away_x = {
        dx: jnp.abs(point_x - (mid_x - at * PX).astype(F32).astype(BF)) * BF(1 / DSTEP)
        for dx, at in ((0, 0), (1, turn), (-1, -turn))
    }
    away_y = {
        dy: jnp.abs(point_y - (mid_y - dy * PY).astype(F32).astype(BF)) * BF(1 / DSTEP) - BF(shift)
        for dy in (-1, 0, 1)
    }

    def migrate(tiles):
        depth = classes_at(*tiles[0]) * nj
        for n, (dx, dy) in enumerate(tiles):
            level = (away_x[dx] + away_y[dy]) + BF(grid)
            entry = (dx * turn + 1) * 3 + (dy + 1)
            live = jnp.concatenate(
                [jnp.full((1, tr), aperture[i, k, entry], jnp.int32) for i, k in blocks], axis=1
            ).astype(F32)
            for d in range(classes_at(dx, dy)):
                amplitude[pl.ds(n * cols, cols), pl.ds(d * nj, nj)] = jnp.where(
                    level == BF(grid + d), (scaled[d] * live).astype(BF), zero
                )
        part = jnp.dot(
            amplitude[pl.ds(0, len(tiles) * cols), pl.ds(0, depth)],
            values[pl.ds(0, depth), :],
            preferred_element_type=F32,
        )
        return [part[n * cols : (n + 1) * cols] for n in range(len(tiles))]

    for n, dx in enumerate((1, -1, 0)):
        for k, part in enumerate(migrate([(dx, -1), (dx, 1)])):
            y_out[n, k] = part.astype(BF)
        if n == 0:
            there = [t.astype(jnp.int32) for t in has_x + has_y]
            pl.semaphore_wait(barrier, sum(there))
        send_y(n)
    for k, part in enumerate(migrate([(1, 0), (-1, 0)])):
        own[k] = part
    own[2] = migrate([(0, 0)])[0]

    def summed(n):
        arrive_y(n)
        return own[n] + y_in[n, 0].astype(F32) + y_in[n, 1].astype(F32)

    for k in range(2):
        x_out[k] = summed(k).astype(BF)
        when(has_x[k], along_x[k].start)
    total[...] = summed(2)
    for k in range(2):
        when(has_x[k], along_x[k].wait_recv)
        from_x[k] = x_in[k]
    for k in range(2):
        for n in range(3):
            when(has_y[k], along_y[n][k].wait_send)
        when(has_x[k], along_x[k].wait_send)


def per_device(n_x, n_y, traces, aperture, geometry, trace_weight, class_weight, traveltime):
    bx, by, tr, ns = traces.shape
    nc, nt = traveltime.shape
    nj = bx * by * tr
    cols = PX * PY
    geometry = jnp.transpose(geometry, (0, 2, 1, 3))
    vmem = pl.BlockSpec(memory_space=pltpu.VMEM)
    total, from_x = pl.pallas_call(
        functools.partial(kernel, n_x, n_y),
        out_shape=(pltpu.VMEM((cols, nt), F32), pltpu.VMEM((2, cols, nt), BF)),
        in_specs=[pl.BlockSpec(memory_space=pltpu.HBM)] * 6,
        out_specs=(vmem, vmem),
        scratch_shapes=[
            pltpu.VMEM(traces.shape, traces.dtype),
            pltpu.VMEM(geometry.shape, geometry.dtype),
            pltpu.VMEM(trace_weight.shape, trace_weight.dtype),
            pltpu.VMEM(traveltime.shape, traveltime.dtype),
            pltpu.SMEM(aperture.shape, aperture.dtype),
            pltpu.SMEM(class_weight.shape, class_weight.dtype),
            pltpu.VMEM((nc, ns, nt), BF),
            pltpu.VMEM((nc, nj, nt), BF),
            pltpu.VMEM((ND * nj, nt), BF),
            pltpu.VMEM((2 * cols, ND * nj), BF),
            pltpu.VMEM((3, cols, nt), F32),
            pltpu.VMEM((3, 2, cols, nt), BF),
            pltpu.VMEM((3, 2, cols, nt), BF),
            pltpu.VMEM((2, cols, nt), BF),
            pltpu.VMEM((2, cols, nt), BF),
            pltpu.SemaphoreType.DMA((6,)),
            pltpu.SemaphoreType.DMA((8,)),
            pltpu.SemaphoreType.DMA((8,)),
        ],
        compiler_params=pltpu.CompilerParams(collective_id=0, has_side_effects=True),
    )(traces, geometry, trace_weight, traveltime, aperture, class_weight)
    image = total + from_x[0].astype(F32) + from_x[1].astype(F32)
    return image.reshape(PX, PY, nt)


def solution(mesh):
    return jax.shard_map(
        functools.partial(per_device, mesh.shape["gx"], mesh.shape["gy"]),
        mesh=mesh,
        in_specs=(
            P("gx", "gy", None, None),
            P("gx", "gy", None),
            P("gx", "gy", None, None),
            P("gx", "gy", None),
            P(),
            P(),
        ),
        out_specs=P("gx", "gy", None),
        check_vma=False,
    )
```

time: 16.4 us -> 13.9 us (0.85)
  local copies, waits for them, and re-layouts: 2.86 us -> 0 us
  other arithmetic: 0 us -> 0.68 us
  Pallas kernels: 13.2 us -> 13 us
    unnamed x2 -> x0, local copies, waits for them, and re-layouts: 2.86 us -> none
    reshape x0 -> x1, other arithmetic: none -> 0.68 us  [per_device(): return image.reshape(PX, PY, nt)]
    pallas_call x1, Pallas kernels: 13.2 us -> 13 us  [per_device(): pl.pallas_call(functools.partial(kernel, n_x, n_y), out_shape=(pltpu.VMEM...]
where the time goes in v2:
time: 13.9 us; the launch traced here: 13.7 us
  Pallas kernels  13 us (94%)
  other arithmetic  0.68 us (5%)
    pallas_call x1, Pallas kernels, per_device(): pl.pallas_call(functools.partial(kernel, n_x, n_y), out_shape=(pltpu.VMEM...  13 us
    reshape x1, other arithmetic, per_device(): return image.reshape(PX, PY, nt)  0.68 us

profile of v2, /device:TPU:1, one launch (start us, length us, event | category | flops | bytes accessed | tf_op | source)
XLA Modules:
  0.0 13.7 jit_solution(2786372452938880969)
XLA Ops:
  0.0 13.0 %shard_map.64 = (f32[128,256]{1,0:T(8,128)S(1)}, bf16[2,128,256]{2,1,0:T(8,128)(2,1)S(1)}) custom-call(bf16[2,2,128,256]{3,2,1,0:T(8,128)(2,1)} %traces_at.1, s32[2,3,2,128]{3,2,1,0:T(2,128)} %bitcast.9, bf16[2,2,128]{2,1,0:T(2,128)(2,1)} %weight_at.1, s32[14,256]{1,0:T(8,128)} %traveltime_at.1, s32[2,2,9]{2,1,0:T(2,128)} %aperture_at.1, f32[14]{0:T(128)} %class_weight_at.1), custom_call_target="tpu_custom_call" | custom-call | tf_op jit(solution)/shard_map/pallas_call | solution.py:238
  13.0 0.7 %fusion = f32[16,8,256]{2,1,0:T(8,128)} fusion(f32[128,256]{1,0:T(8,128)S(1)} %get-tuple-element.7, bf16[2,128,256]{2,1,0:T(8,128)(2,1)S(1)} %get-tuple-element.8), kind=kLoop, calls=%fused_computation.1 | loop fusion | flops 131072 | bytes 393216 | tf_op jit(solution)/shard_map/reshape | solution.py:266

commit v3 on v2

--- a/solution.py
+++ b/solution.py
@@ -73,12 +73,30 @@
             device_id=device, device_id_type=MESH,
         )
 
+    half = cols // 2
+    cuts = [pl.ds(m * half, half) for m in range(2)]
     along_y = [
-        [copy(y_out.at[n, k], y_in.at[n, k], 2 * n + k, {"gy": me_y + step_y[k]}) for k in range(2)]
+        [
+            [
+                copy(
+                    y_out.at[n, k, cut], y_in.at[n, k, cut], 4 * n + 2 * m + k,
+                    {"gy": me_y + step_y[k]},
+                )
+                for k in range(2)
+            ]
+            for m, cut in enumerate(cuts)
+        ]
         for n in range(3)
     ]
     along_x = [
-        copy(x_out.at[k], x_in.at[k], 6 + k, {"gx": me_x + step_x[k]}) for k in range(2)
+        [
+            copy(
+                x_out.at[k, cut], x_in.at[k, cut], 12 + 2 * k + m,
+                {"gx": me_x + step_x[k]},
+            )
+            for m, cut in enumerate(cuts)
+        ]
+        for k in range(2)
     ]
 
     def when(there, act):
@@ -86,11 +104,14 @@
 
     def send_y(n):
         for k in range(2):
-            when(has_y[k], along_y[n][k].start)
-
-    def arrive_y(n):
+            @pl.when(has_y[k])
+            def _(k=k):
+                for m in range(2):
+                    along_y[n][m][k].start()
+
+    def arrive_y(n, m):
         for k in range(2):
-            when(has_y[1 - k], along_y[n][k].wait_recv)
+            when(has_y[1 - k], along_y[n][m][k].wait_recv)
 
     for k in range(2):
         @pl.when(jnp.logical_not(has_y[1 - k]))
@@ -122,11 +143,65 @@
             jnp.where(sample_ids == next_b[c : c + 1, :], frac_b[c : c + 1, :], zero),
         )
 
-    for load in loads[1:]:
+    for load in loads[2:]:
         load.wait()
-    samples = traces[...].reshape(nj, ns)
-    for c in range(nc):
-        taps[c] = jnp.dot(samples, interp[c], preferred_element_type=F32).astype(BF)
+    offset = row(geometry, 2)
+    trace_weight = jnp.concatenate([weight[i, k : k + 1, :] for i, k in blocks], axis=1).astype(F32)
+    scaled = []
+    for d in range(ND):
+        factor = jnp.zeros((1, nj), F32)
+        for h in range(nh):
+            factor = jnp.where(offset == h, class_weight[h + d], factor)
+        scaled.append((trace_weight * factor).astype(BF).astype(F32))
+
+    point = lax.broadcasted_iota(jnp.int32, (cols, nj), 0)
+    point_x = (point // PY).astype(F32).astype(BF)
+    point_y = (point % PY).astype(F32).astype(BF)
+    mid_x = row(geometry, 0) - me_x * PX
+    mid_y = row(geometry, 1) - me_y * PY
+    grid = 136.0
+    shift = (DSTEP - 1) / (2 * DSTEP)
+    away_x = {
+        dx: jnp.abs(point_x - (mid_x - at * PX).astype(F32).astype(BF)) * BF(1 / DSTEP)
+        for dx, at in ((0, 0), (1, turn), (-1, -turn))
+    }
+    away_y = {
+        dy: jnp.abs(point_y - (mid_y - dy * PY).astype(F32).astype(BF)) * BF(1 / DSTEP) - BF(shift)
+        for dy in (-1, 0, 1)
+    }
+
+    def weigh(tiles, top):
+        for n, (dx, dy) in enumerate(tiles):
+            level = (away_x[dx] + away_y[dy]) + BF(grid)
+            entry = (dx * turn + 1) * 3 + (dy + 1)
+            live = jnp.concatenate(
+                [jnp.full((1, tr), aperture[i, k, entry], jnp.int32) for i, k in blocks], axis=1
+            ).astype(F32)
+            for d in range(classes_at(dx, dy)):
+                amplitude[pl.ds((top + n) * cols, cols), pl.ds(d * nj, nj)] = jnp.where(
+                    level == BF(grid + d), (scaled[d] * live).astype(BF), zero
+                )
+
+    def migrate(tiles, top):
+        depth = classes_at(*tiles[0]) * nj
+        part = jnp.dot(
+            amplitude[pl.ds(top * cols, len(tiles) * cols), pl.ds(0, depth)],
+            values[pl.ds(0, depth), :],
+            preferred_element_type=F32,
+        )
+        return [part[n * cols : (n + 1) * cols] for n in range(len(tiles))]
+
+    aside = [[(dx, -1), (dx, 1)] for dx in (1, -1, 0)]
+    weigh(aside[0], 0)
+
+    loads[1].wait()
+    rows_at = nj // 2
+    for start in range(0, nj, rows_at):
+        samples = traces[...].reshape(nj, ns)[start : start + rows_at]
+        for c in range(nc):
+            taps[c, pl.ds(start, rows_at), :] = jnp.dot(
+                samples, interp[c], preferred_element_type=F32
+            ).astype(BF)
 
     for b, (i, k) in enumerate(blocks):
         offset_row = geometry[i, 2, k : k + 1, :].astype(F32)
@@ -156,76 +231,48 @@
                 for n, v in enumerate(value[d]):
                     values[pl.ds(d * nj + b * tr + r, 16), pl.ds(n * tr, tr)] = v
 
-    offset = row(geometry, 2)
-    trace_weight = jnp.concatenate([weight[i, k : k + 1, :] for i, k in blocks], axis=1).astype(F32)
-    scaled = []
-    for d in range(ND):
-        factor = jnp.zeros((1, nj), F32)
-        for h in range(nh):
-            factor = jnp.where(offset == h, class_weight[h + d], factor)
-        scaled.append((trace_weight * factor).astype(BF).astype(F32))
-
-    point = lax.broadcasted_iota(jnp.int32, (cols, nj), 0)
-    point_x = (point // PY).astype(F32).astype(BF)
-    point_y = (point % PY).astype(F32).astype(BF)
-    mid_x = row(geometry, 0) - me_x * PX
-    mid_y = row(geometry, 1) - me_y * PY
-    grid = 136.0
-    shift = (DSTEP - 1) / (2 * DSTEP)
-    away_x = {
-        dx: jnp.abs(point_x - (mid_x - at * PX).astype(F32).astype(BF)) * BF(1 / DSTEP)
-        for dx, at in ((0, 0), (1, turn), (-1, -turn))
-    }
-    away_y = {
-        dy: jnp.abs(point_y - (mid_y - dy * PY).astype(F32).astype(BF)) * BF(1 / DSTEP) - BF(shift)
-        for dy in (-1, 0, 1)
-    }
-
-    def migrate(tiles):
-        depth = classes_at(*tiles[0]) * nj
-        for n, (dx, dy) in enumerate(tiles):
-            level = (away_x[dx] + away_y[dy]) + BF(grid)
-            entry = (dx * turn + 1) * 3 + (dy + 1)
-            live = jnp.concatenate(
-                [jnp.full((1, tr), aperture[i, k, entry], jnp.int32) for i, k in blocks], axis=1
-            ).astype(F32)
-            for d in range(classes_at(dx, dy)):
-                amplitude[pl.ds(n * cols, cols), pl.ds(d * nj, nj)] = jnp.where(
-                    level == BF(grid + d), (scaled[d] * live).astype(BF), zero
-                )
-        part = jnp.dot(
-            amplitude[pl.ds(0, len(tiles) * cols), pl.ds(0, depth)],
-            values[pl.ds(0, depth), :],
-            preferred_element_type=F32,
-        )
-        return [part[n * cols : (n + 1) * cols] for n in range(len(tiles))]
-
-    for n, dx in enumerate((1, -1, 0)):
-        for k, part in enumerate(migrate([(dx, -1), (dx, 1)])):
+    for n, tiles in enumerate(aside):
+        if n:
+            weigh(tiles, 2 * n)
+        for k, part in enumerate(migrate(tiles, 2 * n)):
             y_out[n, k] = part.astype(BF)
         if n == 0:
             there = [t.astype(jnp.int32) for t in has_x + has_y]
             pl.semaphore_wait(barrier, sum(there))
         send_y(n)
-    for k, part in enumerate(migrate([(1, 0), (-1, 0)])):
+    along = [(1, 0), (-1, 0)]
+    weigh(along, 6)
+    weigh([(0, 0)], 8)
+    for k, part in enumerate(migrate(along, 6)):
         own[k] = part
-    own[2] = migrate([(0, 0)])[0]
-
-    def summed(n):
-        arrive_y(n)
-        return own[n] + y_in[n, 0].astype(F32) + y_in[n, 1].astype(F32)
-
-    for k in range(2):
-        x_out[k] = summed(k).astype(BF)
-        when(has_x[k], along_x[k].start)
-    total[...] = summed(2)
-    for k in range(2):
-        when(has_x[k], along_x[k].wait_recv)
-        from_x[k] = x_in[k]
-    for k in range(2):
-        for n in range(3):
-            when(has_y[k], along_y[n][k].wait_send)
-        when(has_x[k], along_x[k].wait_send)
+    own[2] = migrate([(0, 0)], 8)[0]
+
+    def summed(n, m):
+        cut = cuts[m]
+        arrive_y(n, m)
+        return own[n, cut] + y_in[n, 0, cut].astype(F32) + y_in[n, 1, cut].astype(F32)
+
+    for k in range(2):
+        for m, cut in enumerate(cuts):
+            x_out[k, cut] = summed(k, m).astype(BF)
+            when(has_x[k], along_x[k][m].start)
+    for m, cut in enumerate(cuts):
+        total[cut] = summed(2, m)
+    for k in range(2):
+        for m, cut in enumerate(cuts):
+            when(has_x[k], along_x[k][m].wait_recv)
+            from_x[k, cut] = x_in[k, cut]
+    for k in range(2):
+        @pl.when(has_y[k])
+        def _(k=k):
+            for n in range(3):
+                for m in range(2):
+                    along_y[n][m][k].wait_send()
+
+        @pl.when(has_x[k])
+        def _(k=k):
+            for m in range(2):
+                along_x[k][m].wait_send()
 
 
 def per_device(n_x, n_y, traces, aperture, geometry, trace_weight, class_weight, traveltime):
@@ -250,15 +297,15 @@
             pltpu.VMEM((nc, ns, nt), BF),
             pltpu.VMEM((nc, nj, nt), BF),
             pltpu.VMEM((ND * nj, nt), BF),
-            pltpu.VMEM((2 * cols, ND * nj), BF),
+            pltpu.VMEM((9 * cols, ND * nj), BF),
             pltpu.VMEM((3, cols, nt), F32),
             pltpu.VMEM((3, 2, cols, nt), BF),
             pltpu.VMEM((3, 2, cols, nt), BF),
             pltpu.VMEM((2, cols, nt), BF),
             pltpu.VMEM((2, cols, nt), BF),
             pltpu.SemaphoreType.DMA((6,)),
-            pltpu.SemaphoreType.DMA((8,)),
-            pltpu.SemaphoreType.DMA((8,)),
+            pltpu.SemaphoreType.DMA((16,)),
+            pltpu.SemaphoreType.DMA((16,)),
         ],
         compiler_params=pltpu.CompilerParams(collective_id=0, has_side_effects=True),
     )(traces, geometry, trace_weight, traveltime, aperture, class_weight)

time: 13.9 us -> 14.7 us (1.058)
  the two profiles are of different devices: /device:TPU:1 before, /device:TPU:0 now
where the time goes in v3:
time: 14.7 us; the launch traced here: 14.5 us
  Pallas kernels  13.8 us (94%)
  other arithmetic  0.68 us (5%)
    pallas_call x1, Pallas kernels, per_device(): pl.pallas_call(functools.partial(kernel, n_x, n_y), out_shape=(pltpu.VMEM...  13.8 us
    reshape x1, other arithmetic, per_device(): return image.reshape(PX, PY, nt)  0.68 us

profile of v3, /device:TPU:0, one launch (start us, length us, event | category | flops | bytes accessed | tf_op | source)
XLA Modules:
  0.0 14.5 jit_solution(7975979831998300775)
XLA Ops:
  0.0 13.8 %shard_map.64 = (f32[128,256]{1,0:T(8,128)S(1)}, bf16[2,128,256]{2,1,0:T(8,128)(2,1)S(1)}) custom-call(bf16[2,2,128,256]{3,2,1,0:T(8,128)(2,1)} %traces_at.1, s32[2,3,2,128]{3,2,1,0:T(2,128)} %bitcast.9, bf16[2,2,128]{2,1,0:T(2,128)(2,1)} %weight_at.1, s32[14,256]{1,0:T(8,128)} %traveltime_at.1, s32[2,2,9]{2,1,0:T(2,128)} %aperture_at.1, f32[14]{0:T(128)} %class_weight_at.1), custom_call_target="tpu_custom_call" | custom-call | tf_op jit(solution)/shard_map/pallas_call | solution.py:285
  13.8 0.7 %fusion = f32[16,8,256]{2,1,0:T(8,128)} fusion(f32[128,256]{1,0:T(8,128)S(1)} %get-tuple-element.7, bf16[2,128,256]{2,1,0:T(8,128)(2,1)S(1)} %get-tuple-element.8), kind=kLoop, calls=%fused_computation.1 | loop fusion | flops 131072 | bytes 393216 | tf_op jit(solution)/shard_map/reshape | solution.py:313

commit v4 on v2

--- a/solution.py
+++ b/solution.py
@@ -73,12 +73,30 @@
             device_id=device, device_id_type=MESH,
         )
 
+    half = cols // 2
+    cuts = [pl.ds(m * half, half) for m in range(2)]
     along_y = [
-        [copy(y_out.at[n, k], y_in.at[n, k], 2 * n + k, {"gy": me_y + step_y[k]}) for k in range(2)]
+        [
+            [
+                copy(
+                    y_out.at[n, k, cut], y_in.at[n, k, cut], 4 * n + 2 * m + k,
+                    {"gy": me_y + step_y[k]},
+                )
+                for k in range(2)
+            ]
+            for m, cut in enumerate(cuts)
+        ]
         for n in range(3)
     ]
     along_x = [
-        copy(x_out.at[k], x_in.at[k], 6 + k, {"gx": me_x + step_x[k]}) for k in range(2)
+        [
+            copy(
+                x_out.at[k, cut], x_in.at[k, cut], 12 + 2 * k + m,
+                {"gx": me_x + step_x[k]},
+            )
+            for m, cut in enumerate(cuts)
+        ]
+        for k in range(2)
     ]
 
     def when(there, act):
@@ -86,11 +104,14 @@
 
     def send_y(n):
         for k in range(2):
-            when(has_y[k], along_y[n][k].start)
-
-    def arrive_y(n):
+            @pl.when(has_y[k])
+            def _(k=k):
+                for m in range(2):
+                    along_y[n][m][k].start()
+
+    def arrive_y(n, m):
         for k in range(2):
-            when(has_y[1 - k], along_y[n][k].wait_recv)
+            when(has_y[1 - k], along_y[n][m][k].wait_recv)
 
     for k in range(2):
         @pl.when(jnp.logical_not(has_y[1 - k]))
@@ -211,21 +232,32 @@
         own[k] = part
     own[2] = migrate([(0, 0)])[0]
 
-    def summed(n):
-        arrive_y(n)
-        return own[n] + y_in[n, 0].astype(F32) + y_in[n, 1].astype(F32)
-
-    for k in range(2):
-        x_out[k] = summed(k).astype(BF)
-        when(has_x[k], along_x[k].start)
-    total[...] = summed(2)
-    for k in range(2):
-        when(has_x[k], along_x[k].wait_recv)
-        from_x[k] = x_in[k]
-    for k in range(2):
-        for n in range(3):
-            when(has_y[k], along_y[n][k].wait_send)
-        when(has_x[k], along_x[k].wait_send)
+    def summed(n, m):
+        cut = cuts[m]
+        arrive_y(n, m)
+        return own[n, cut] + y_in[n, 0, cut].astype(F32) + y_in[n, 1, cut].astype(F32)
+
+    for k in range(2):
+        for m, cut in enumerate(cuts):
+            x_out[k, cut] = summed(k, m).astype(BF)
+            when(has_x[k], along_x[k][m].start)
+    for m, cut in enumerate(cuts):
+        total[cut] = summed(2, m)
+    for k in range(2):
+        for m, cut in enumerate(cuts):
+            when(has_x[k], along_x[k][m].wait_recv)
+            from_x[k, cut] = x_in[k, cut]
+    for k in range(2):
+        @pl.when(has_y[k])
+        def _(k=k):
+            for n in range(3):
+                for m in range(2):
+                    along_y[n][m][k].wait_send()
+
+        @pl.when(has_x[k])
+        def _(k=k):
+            for m in range(2):
+                along_x[k][m].wait_send()
 
 
 def per_device(n_x, n_y, traces, aperture, geometry, trace_weight, class_weight, traveltime):
@@ -257,8 +289,8 @@
             pltpu.VMEM((2, cols, nt), BF),
             pltpu.VMEM((2, cols, nt), BF),
             pltpu.SemaphoreType.DMA((6,)),
-            pltpu.SemaphoreType.DMA((8,)),
-            pltpu.SemaphoreType.DMA((8,)),
+            pltpu.SemaphoreType.DMA((16,)),
+            pltpu.SemaphoreType.DMA((16,)),
         ],
         compiler_params=pltpu.CompilerParams(collective_id=0, has_side_effects=True),
     )(traces, geometry, trace_weight, traveltime, aperture, class_weight)

time: 13.9 us -> 14.4 us (1.036)
  the two profiles are of different devices: /device:TPU:1 before, /device:TPU:0 now
where the time goes in v4:
time: 14.4 us; the launch traced here: 14.2 us
  Pallas kernels  13.5 us (94%)
  other arithmetic  0.68 us (5%)
    pallas_call x1, Pallas kernels, per_device(): pl.pallas_call(functools.partial(kernel, n_x, n_y), out_shape=(pltpu.VMEM...  13.5 us
    reshape x1, other arithmetic, per_device(): return image.reshape(PX, PY, nt)  0.68 us

profile of v4, /device:TPU:0, one launch (start us, length us, event | category | flops | bytes accessed | tf_op | source)
XLA Modules:
  0.0 14.2 jit_solution(14241914941875652688)
XLA Ops:
  0.0 13.5 %shard_map.64 = (f32[128,256]{1,0:T(8,128)S(1)}, bf16[2,128,256]{2,1,0:T(8,128)(2,1)S(1)}) custom-call(bf16[2,2,128,256]{3,2,1,0:T(8,128)(2,1)} %traces_at.1, s32[2,3,2,128]{3,2,1,0:T(2,128)} %bitcast.9, bf16[2,2,128]{2,1,0:T(2,128)(2,1)} %weight_at.1, s32[14,256]{1,0:T(8,128)} %traveltime_at.1, s32[2,2,9]{2,1,0:T(2,128)} %aperture_at.1, f32[14]{0:T(128)} %class_weight_at.1), custom_call_target="tpu_custom_call" | custom-call | tf_op jit(solution)/shard_map/pallas_call | solution.py:270
  13.5 0.7 %fusion = f32[16,8,256]{2,1,0:T(8,128)} fusion(f32[128,256]{1,0:T(8,128)S(1)} %get-tuple-element.7, bf16[2,128,256]{2,1,0:T(8,128)(2,1)S(1)} %get-tuple-element.8), kind=kLoop, calls=%fused_computation.1 | loop fusion | flops 131072 | bytes 393216 | tf_op jit(solution)/shard_map/reshape | solution.py:298
